TPU v7x, 32 devices: a whole 2x2x4 slice. The times are simulated.
32 devices in a mesh: row: 8 (over z, x), col: 4 (over y, core).
Axes of the slice: x: 2, y: 2, z: 4, core: 2. Of those that a mesh axis runs over, the one named last changes fastest.
Arguments:
- offsets: int32 [8, 4, 2], P('row', 'col'), may hold values from 1 to 3
- targets: float32 [3, 3, 256, 512], P(None, None, 'row', 'col'), may hold values from -60 to 60
- grid_fine: float32 [32, 256, 512], P(None, 'row', 'col'), may hold values from -6 to 6
- grid_coarse: float32 [32, 64, 128], P(None, 'row', 'col'), may hold values from -6 to 6
- weight_in: float32 [512, 64], replicated, may hold values from -0.75 to 0.75
- weight_mid: float32 [1, 512, 512], replicated, may hold values from -0.25 to 0.25
- weight_out: float32 [3, 512], replicated, may hold values from -0.397747564 to 0.397747564
- fine_first: float32 [32, 256, 512], P(None, 'row', 'col'), may hold values from -0.012 to 0.012
- fine_second: float32 [32, 256, 512], P(None, 'row', 'col'), may hold values from 1e-06 to 0.0001
- coarse_first: float32 [32, 64, 128], P(None, 'row', 'col'), may hold values from -0.012 to 0.012
- coarse_second: float32 [32, 64, 128], P(None, 'row', 'col'), may hold values from 1e-06 to 0.0001
- in_first: float32 [512, 64], replicated, may hold values from -0.012 to 0.012
- in_second: float32 [512, 64], replicated, may hold values from 1e-06 to 0.0001
- mid_first: float32 [1, 512, 512], replicated, may hold values from -0.012 to 0.012
- mid_second: float32 [1, 512, 512], replicated, may hold values from 1e-06 to 0.0001
- out_first: float32 [3, 512], replicated, may hold values from -0.012 to 0.012
- out_second: float32 [3, 512], replicated, may hold values from 1e-06 to 0.0001
Outputs:
- fine_step: float32 [32, 256, 512], P(None, 'row', 'col')
- coarse_step: float32 [32, 64, 128], P(None, 'row', 'col')
- input_step: float32 [512, 64], replicated
- middle_step: float32 [1, 512, 512], replicated
- output_step: float32 [3, 512], replicated
All inputs are finite; a program needn't handle non-finite values.
Results may differ from a plain program's by a relative error of at most 0.0014.
The roundings to bfloat16 on the way count: a program that leaves them out, or rounds other values in their place, can miss the bound.
Values sent between devices are 32-bit elements; how exact they have to be, the bound alone decides.
A program may use at most 64 MiB of HBM per device.

v0:
```python
import jax
import jax.numpy as jnp
from jax import lax
from jax.sharding import PartitionSpec as P

SUB = 4
RATIO = 4
ADAM_STEP = 10
BETA_ONE = 0.9
BETA_TWO = 0.99
ADAM_EPSILON = 1e-08
CLIP_RMS = 0.01
LOSS_VALUE = 0.25
MEAN_EPSILON = 1e-06


def shifted(block, axis, distance):
    devices = range(lax.axis_size(axis))
    route = [(i - distance, i) for i in devices if i - distance in devices]
    return lax.ppermute(block, axis, route)


def interp_table(samples, level_ratio, offset):
    positions = jnp.arange(samples, dtype=jnp.int32)
    base_index = positions // level_ratio
    fraction = (
        (positions % level_ratio).astype(jnp.float32) + offset.astype(jnp.float32) / SUB
    ) / level_ratio
    column = jnp.arange(samples // level_ratio + 1, dtype=jnp.int32)
    lower_hit = (column[None, :] == base_index[:, None]).astype(jnp.float32)
    upper_hit = (column[None, :] == base_index[:, None] + 1).astype(jnp.float32)
    return lower_hit * (1.0 - fraction)[:, None] + upper_hit * fraction[:, None]


def level_tables(row_count, col_count, shift_y, shift_x):
    return (
        interp_table(row_count, 1, shift_y),
        interp_table(col_count, 1, shift_x),
        interp_table(row_count, RATIO, shift_y),
        interp_table(col_count, RATIO, shift_x),
    )


def sample_level(extended, row_table, col_table):
    across = jnp.einsum("kjl,ml->kjm", extended, col_table, precision=lax.Precision.HIGHEST)
    return jnp.einsum("ij,kjm->kim", row_table, across, precision=lax.Precision.HIGHEST)


def spread_level(cotangent, row_table, col_table):
    backward = jnp.einsum("ij,kim->kjm", row_table, cotangent, precision=lax.Precision.HIGHEST)
    return jnp.einsum("kjm,ml->kjl", backward, col_table, precision=lax.Precision.HIGHEST)


def sample_features(fine_ext, coarse_ext, tables):
    fine_feat = sample_level(fine_ext, tables[0], tables[1])
    coarse_feat = sample_level(coarse_ext, tables[2], tables[3])
    channels, row_count, col_count = fine_feat.shape
    return jnp.concatenate(
        [
            fine_feat.reshape(channels, row_count * col_count),
            coarse_feat.reshape(channels, row_count * col_count),
        ],
        axis=0,
    ).astype(jnp.bfloat16)


def spread_features(feature_grad, tables):
    channels = feature_grad.shape[0] // 2
    row_count = tables[0].shape[0]
    col_count = tables[1].shape[0]
    fine_cot = feature_grad[:channels].reshape(channels, row_count, col_count)
    coarse_cot = feature_grad[channels:].reshape(channels, row_count, col_count)
    return (
        spread_level(fine_cot, tables[0], tables[1]),
        spread_level(coarse_cot, tables[2], tables[3]),
    )


def matmul(former, latter):
    return jnp.dot(former, latter, preferred_element_type=jnp.float32)


def contract_rows(former, latter):
    return lax.dot_general(
        former, latter, (((0,), (0,)), ((), ())), preferred_element_type=jnp.float32
    )


def contract_cols(former, latter):
    return lax.dot_general(
        former, latter, (((1,), (1,)), ((), ())), preferred_element_type=jnp.float32
    )


def silu_slope(pre_act):
    sigmoid = jax.nn.sigmoid(pre_act)
    return sigmoid * (1.0 + pre_act * (1.0 - sigmoid))


def decoder_forward(features, low_in, low_mid, low_out):
    pre_acts = [matmul(low_in, features)]
    activations = [jax.nn.silu(pre_acts[0]).astype(jnp.bfloat16)]
    pre_acts.append(matmul(low_mid[0], activations[-1]))
    activations.append(jax.nn.silu(pre_acts[-1]).astype(jnp.bfloat16))
    return (matmul(low_out, activations[-1]), pre_acts, activations)


def decoder_backward(features, pre_acts, activations, cotangent, low_in, low_mid, low_out):
    out_cotangent = cotangent.astype(jnp.bfloat16)
    grad_out = contract_cols(out_cotangent, activations[-1])
    upward = contract_rows(low_out, out_cotangent)
    grads_mid = []
    delta_low = (upward * silu_slope(pre_acts[1])).astype(jnp.bfloat16)
    grads_mid.insert(0, contract_cols(delta_low, activations[0]))
    upward = contract_rows(low_mid[0], delta_low)
    delta_low = (upward * silu_slope(pre_acts[0])).astype(jnp.bfloat16)
    grad_in = contract_cols(delta_low, features)
    feature_grad = contract_rows(low_in, delta_low)
    return (grad_in, jnp.stack(grads_mid), grad_out, feature_grad)


def pixel_cotangent(value_error, row_error, row_prior, col_error, col_prior):
    return (
        2.0 * LOSS_VALUE * value_error
        + 2.0 * (row_prior - row_error)
        + 2.0 * (col_prior - col_error)
    )


def clip_factor(total, entries):
    return jnp.minimum(1.0, CLIP_RMS / jnp.sqrt(total / entries + MEAN_EPSILON))


def adam_step(gradient, moment_one, moment_two, clip_scale):
    clipped = gradient * clip_scale
    new_one = BETA_ONE * moment_one + (1.0 - BETA_ONE) * clipped
    new_two = BETA_TWO * moment_two + (1.0 - BETA_TWO) * clipped * clipped
    return (
        new_one
        / (1.0 - BETA_ONE**ADAM_STEP)
        / (jnp.sqrt(new_two / (1.0 - BETA_TWO**ADAM_STEP)) + ADAM_EPSILON)
    )


def grid_total_sum(grid_local):
    return lax.psum(grid_local, ("row", "col"))


def shards(
    offsets,
    targets,
    grid_fine,
    grid_coarse,
    weight_in,
    weight_mid,
    weight_out,
    fine_first,
    fine_second,
    coarse_first,
    coarse_second,
    in_first,
    in_second,
    mid_first,
    mid_second,
    out_first,
    out_second,
):
    channels, sample_rows, sample_cols = grid_fine.shape
    coarse_rows = grid_coarse.shape[1]
    coarse_cols = grid_coarse.shape[2]
    low_in = weight_in.astype(jnp.bfloat16)
    low_mid = weight_mid.astype(jnp.bfloat16)
    low_out = weight_out.astype(jnp.bfloat16)
    top_rows = jnp.concatenate([grid_fine[:, :1, :], grid_coarse[:, :1, :]], axis=2)
    top_rows = shifted(top_rows, "row", -1)
    fine_tall = jnp.concatenate([grid_fine, top_rows[:, :, :sample_cols]], axis=1)
    coarse_tall = jnp.concatenate([grid_coarse, top_rows[:, :, sample_cols:]], axis=1)
    edge_cols = jnp.concatenate([fine_tall[:, :, :1], coarse_tall[:, :, :1]], axis=1)
    edge_cols = shifted(edge_cols, "col", -1)
    fine_ext = jnp.concatenate([fine_tall, edge_cols[:, : sample_rows + 1, :]], axis=2)
    coarse_ext = jnp.concatenate([coarse_tall, edge_cols[:, sample_rows + 1 :, :]], axis=2)
    tables = level_tables(sample_rows, sample_cols, offsets[0, 0, 0], offsets[0, 0, 1])
    features = sample_features(fine_ext, coarse_ext, tables)
    predicted, pre_acts, activations = decoder_forward(features, low_in, low_mid, low_out)
    outputs = predicted.shape[0]
    predicted = predicted.reshape(outputs, sample_rows, sample_cols)
    below = shifted(predicted[:, :1, :], "row", -1)
    beside = shifted(predicted[:, :, :1], "col", -1)
    row_global = lax.axis_index("row") * sample_rows + jnp.arange(sample_rows, dtype=jnp.int32)
    col_global = lax.axis_index("col") * sample_cols + jnp.arange(sample_cols, dtype=jnp.int32)
    row_valid = (row_global < lax.axis_size("row") * sample_rows - 1)[None, :, None]
    col_valid = (col_global < lax.axis_size("col") * sample_cols - 1)[None, None, :]
    row_next = jnp.concatenate([predicted[:, 1:, :], below], axis=1)
    col_next = jnp.concatenate([predicted[:, :, 1:], beside], axis=2)
    value_error = predicted - targets[0]
    row_error = jnp.where(row_valid, row_next - predicted - targets[1], 0.0)
    col_error = jnp.where(col_valid, col_next - predicted - targets[2], 0.0)
    above = shifted(row_error[:, -1:, :], "row", 1)
    before = shifted(col_error[:, :, -1:], "col", 1)
    row_prior = jnp.concatenate([above, row_error[:, :-1, :]], axis=1)
    col_prior = jnp.concatenate([before, col_error[:, :, :-1]], axis=2)
    cotangent = pixel_cotangent(value_error, row_error, row_prior, col_error, col_prior)
    grad_in, grad_mid, grad_out, feature_grad = decoder_backward(
        features,
        pre_acts,
        activations,
        cotangent.reshape(outputs, sample_rows * sample_cols),
        low_in,
        low_mid,
        low_out,
    )
    fine_back, coarse_back = spread_features(feature_grad, tables)
    side_cols = jnp.concatenate(
        [fine_back[:, :, sample_cols:], coarse_back[:, :, coarse_cols:]], axis=1
    )
    side_cols = shifted(side_cols, "col", 1)
    fine_tall_grad = jnp.concatenate(
        [fine_back[:, :, :1] + side_cols[:, : sample_rows + 1, :], fine_back[:, :, 1:sample_cols]],
        axis=2,
    )
    coarse_tall_grad = jnp.concatenate(
        [
            coarse_back[:, :, :1] + side_cols[:, sample_rows + 1 :, :],
            coarse_back[:, :, 1:coarse_cols],
        ],
        axis=2,
    )
    bottom_rows = jnp.concatenate(
        [fine_tall_grad[:, sample_rows:, :], coarse_tall_grad[:, coarse_rows:, :]], axis=2
    )
    bottom_rows = shifted(bottom_rows, "row", 1)
    fine_grad = jnp.concatenate(
        [
            fine_tall_grad[:, :1, :] + bottom_rows[:, :, :sample_cols],
            fine_tall_grad[:, 1:sample_rows, :],
        ],
        axis=1,
    )
    coarse_grad = jnp.concatenate(
        [
            coarse_tall_grad[:, :1, :] + bottom_rows[:, :, sample_cols:],
            coarse_tall_grad[:, 1:coarse_rows, :],
        ],
        axis=1,
    )
    grid_local = jnp.sum(fine_grad * fine_grad) + jnp.sum(coarse_grad * coarse_grad)
    devices = lax.axis_size("row") * lax.axis_size("col")
    grid_entries = (fine_grad.size + coarse_grad.size) * devices
    decoder_entries = weight_in.size + weight_mid.size + weight_out.size
    grad_in, grad_mid, grad_out = lax.psum((grad_in, grad_mid, grad_out), ("row", "col"))
    grid_total = grid_total_sum(grid_local)
    decoder_total = (
        jnp.sum(grad_in * grad_in) + jnp.sum(grad_mid * grad_mid) + jnp.sum(grad_out * grad_out)
    )
    decoder_scale = clip_factor(decoder_total, decoder_entries)
    middle_step = adam_step(grad_mid, mid_first, mid_second, decoder_scale)
    grid_scale = clip_factor(grid_total, grid_entries)
    fine_step = adam_step(fine_grad, fine_first, fine_second, grid_scale)
    coarse_step = adam_step(coarse_grad, coarse_first, coarse_second, grid_scale)
    input_step = adam_step(grad_in, in_first, in_second, decoder_scale)
    output_step = adam_step(grad_out, out_first, out_second, decoder_scale)
    return (fine_step, coarse_step, input_step, middle_step, output_step)


def solution(mesh):
    placed = (
        P("row", "col", None),
        P(None, None, "row", "col"),
        P(None, "row", "col"),
        P(None, "row", "col"),
        P(),
        P(),
        P(),
        P(None, "row", "col"),
        P(None, "row", "col"),
        P(None, "row", "col"),
        P(None, "row", "col"),
        P(),
        P(),
        P(),
        P(),
        P(),
        P(),
    )
    return jax.shard_map(
        shards,
        mesh=mesh,
        in_specs=placed,
        out_specs=(P(None, "row", "col"), P(None, "row", "col"), P(), P(), P()),
        check_vma=False,
    )
```

profile of v0, /device:TPU:0, one launch (start us, length us, event | category | flops | bytes accessed | tf_op | source)
XLA Modules:
  0.0 238.9 jit_solution(828096831755790455)
XLA Ops:
  9.2 1.3 collective-permute-start
  10.5 1.3 fusion.148
  14.0 1.9 collective-permute-done
  17.8 1.3 collective-permute-start.1
  19.1 1.8 collective-permute-done.1
  21.6 2.2 fusion.14
  25.6 1.3 fusion.82
  26.9 4.4 %fusion.5 = (bf16[512,4096]{0,1:T(8,128)(2,1)S(1)}, f32[4096,512]{1,0:T(8,128)S(1)}) fusion(f32[1,512,512]{2,1,0:T(8,128)S(1)} %copy-done.11, f32[4096,512]{1,0:T(8,128)S(1)} %fusion.82), kind=kOutput, calls=%fused_computation.10 | convolution fusion | flops 2168717312 | bytes 22020096 | tf_op jit(solution)/shard_map/dot_general | solution.py:80
  32.6 1.3 collective-permute-start.2
  33.9 1.3 collective-permute-start.4
  35.3 3.6 %collective-permute-done.4 = f32[3,32,1]{2,1,0:T(8,128)S(1)} collective-permute-done((f32[3,32,1]{2,1,0:T(8,128)S(1)}, f32[3,32,1]{2,1,0:T(8,128)S(1)}, u32[]{:S(2)}, u32[]{:S(2)}) %collective-permute-start.4) | collective-permute-done | bytes 416 | tf_op jit(solution)/shard_map/ppermute | solution.py:20
  39.1 4.6 %collective-permute-start.5 = (f32[3,32,1]{2,1,0:T(8,128)S(1)}, f32[3,32,1]{2,1,0:T(8,128)S(1)}, u32[]{:S(2)}, u32[]{:S(2)}) collective-permute-start(f32[3,32,1]{2,1,0:T(8,128)S(1)} %slice.167), channel_id=1, source_target_pairs={{0,1},{1,2},{2,3},{4,5},{5,6},{6,7},{8,9},{9,10},{10,11},{12,13},{... | collective-permute-start | bytes 1160 | tf_op jit(solution)/shard_map/ppermute | solution.py:20
  43.8 5.1 %collective-permute-start.3 = (f32[3,1,128]{2,1,0:T(1,128)S(1)}, f32[3,1,128]{2,1,0:T(1,128)S(1)}, u32[]{:S(2)}, u32[]{:S(2)}) collective-permute-start(f32[3,1,128]{2,1,0:T(1,128)S(1)} %slice.163), channel_id=1, source_target_pairs={{0,4},{4,8},{8,12},{12,16},{16,20},{20,24},{24,28},{1,5},{5,9},{9,... | collective-permute-start | bytes 4616 | tf_op jit(solution)/shard_map/ppermute | solution.py:20
  50.3 3.5 %fusion.1 = bf16[512,4096]{0,1:T(8,128)(2,1)S(1)} fusion(f32[4096,512]{1,0:T(8,128)S(1)} %get-tuple-element.27, bf16[3,4096]{1,0:T(4,128)(2,1)S(1)} %fusion.63, f32[3,512]{1,0:T(4,128)S(1)} %copy-done.8), kind=kOutput, calls=%fused_computation.3 | convolution fusion | flops 31458816 | bytes 12613632 | tf_op jit(solution)/shard_map/dot_general | solution.py:84
  53.8 3.4 %convolution_bitcast_fusion.1 = f32[1,512,512]{2,1,0:T(8,128)} fusion(bf16[512,4096]{0,1:T(8,128)(2,1)S(1)} %fusion.1, f32[4096,512]{1,0:T(8,128)S(1)} %fusion.82), kind=kOutput, calls=%fused_computation.24 | convolution fusion | flops 2157969408 | bytes 13631488 | tf_op jit(solution)/shard_map/dot_general | solution.py:90
  57.3 3.6 %fusion = bf16[512,4096]{0,1:T(8,128)(2,1)S(1)} fusion(f32[4096,512]{1,0:T(8,128)S(1)} %fusion.82, bf16[512,4096]{0,1:T(8,128)(2,1)S(1)} %fusion.1, f32[1,512,512]{2,1,0:T(8,128)S(1)} %copy-done.11), kind=kOutput, calls=%fused_computation.1 | convolution fusion | flops 2166620160 | bytes 17825792 | tf_op jit(solution)/shard_map/dot_general | solution.py:84
  60.9 2.0 copy-done.1
  62.8 1.4 convolution_bitcast_fusion
  67.0 1.2 fusion.56
  68.7 1.3 collective-permute-start.6
  70.0 3.7 %fusion.150 = f32[512,64]{0,1:T(8,128)} fusion(bf16[64,4096]{1,0:T(8,128)(2,1)S(1)} %bitcast_dynamic-update-slice_fusion, bf16[512,4096]{0,1:T(8,128)(2,1)} %copy-done.1), kind=kOutput, calls=%fused_computation.235 | convolution fusion | flops 268435456 | bytes 4849664 | tf_op jit(solution)/shard_map/dot_general | solution.py:90
  74.1 1.2 copy.74
  76.6 4.9 %collective-permute-start.7 = (f32[32,1,160]{2,1,0:T(1,128)S(1)}, f32[32,1,160]{2,1,0:T(1,128)S(1)}, u32[]{:S(2)}, u32[]{:S(2)}) collective-permute-start(f32[32,1,160]{2,1,0:T(1,128)S(1)} %fusion.80), channel_id=1, source_target_pairs={{0,4},{4,8},{8,12},{12,16},{16,20},{20,24},{24,28},{1,5},{5,9},{9,... | collective-permute-start | bytes 61448 | tf_op jit(solution)/shard_map/ppermute | solution.py:20
  81.5 2.8 %fusion.149 = f32[3,512]{1,0:T(4,128)S(1)} fusion(bf16[3,4096]{1,0:T(4,128)(2,1)S(1)} %fusion.63, bf16[512,4096]{0,1:T(8,128)(2,1)} %copy-done), kind=kOutput, calls=%fused_computation.234 | convolution fusion | flops 12582912 | bytes 4225024 | tf_op jit(solution)/shard_map/dot_general | solution.py:90
  87.4 41.9 %all-reduce = (f32[]{:T(128)}, f32[3,512]{1,0:T(4,128)S(1)}) all-reduce(f32[]{:T(128)S(6)} %add.300, f32[3,512]{1,0:T(4,128)S(1)} %fusion.149), channel_id=1, replica_groups=mesh['row'=8,'col'=4] {'row','col'}, use_global_device_ids=true, to_apply=%region_2.3 | all-reduce | flops 1537 | bytes 12296 | tf_op jit(solution)/shard_map/psum | solution.py:146
  130.6 1.7 fusion.49
  132.3 2.5 %fusion.29 = f32[32,32,128]{2,1,0:T(8,128)} fusion(f32[32,32,128]{2,1,0:T(8,128)} %param.25, f32[32,32,128]{2,1,0:T(8,128)} %param.24, f32[]{:T(128)S(6)} %min.6, f32[32,33,127]{2,1,0:T(8,128)S(1)} %slice.175, f32[32,33,1]{2,1,0:T(8,128)S(1)} %copy.72, f32[32,1,128]{2,1,0:T(1,128)S(1)} %slice_add_fusion.1), kind=kLoop, calls=%fused_computation.47 | loop fusion | flops 2228224 | bytes 2129924 | tf_op jit(solution)/shard_map/div | solution.py:139
  134.7 86.2 %all-reduce.4.cloned.1.call-done = (f32[512,64]{0,1:T(8,128)}, f32[1,512,512]{2,1,0:T(8,128)}) async-done(((f32[512,64]{0,1:T(8,128)}, f32[1,512,512]{2,1,0:T(8,128)}), (f32[512,64]{0,1:T(8,128)}, f32[1,512,512]{2,1,0:T(8,128)})) %all-reduce.4.cloned.1.call-update) | async-done | bytes 1179664 | tf_op jit(solution)/shard_map/psum | solution.py:250
  220.9 2.1 multiply_reduce_fusion
  223.0 1.5 multiply_reduce_fusion.2
  227.2 3.2 %fusion.24 = f32[1,512,512]{2,1,0:T(8,128)} fusion(f32[1,512,512]{2,1,0:T(8,128)S(1)} %copy-done.2, f32[1,512,512]{2,1,0:T(8,128)} %get-tuple-element.8, f32[1,512,512]{2,1,0:T(8,128)} %param.30, f32[]{:T(128)S(6)} %min.7), kind=kLoop, calls=%fused_computation.39 | loop fusion | flops 3145728 | bytes 4194308 | tf_op jit(solution)/shard_map/div | solution.py:139
  230.4 1.7 fusion.54
  (97 shorter events, 18.1 us)
Async XLA Ops:
  7.2 18.5 %copy-start.3 = (f32[512,64]{0,1:T(8,128)S(1)}, f32[512,64]{0,1:T(8,128)}, u32[]{:S(2)}) copy-start(f32[512,64]{0,1:T(8,128)} %param.21) | copy-start | bytes 393220
  7.2 213.8 %all-reduce.4.cloned.1.call-start = ((), (), s32[]{:S(2)}) async-start(), calls=%async_computation | async-start | bytes 2359296 | tf_op jit(solution)/shard_map/psum | solution.py:250
  9.2 6.8 %collective-permute-start = (f32[32,1,160]{2,1,0:T(1,128)S(1)}, f32[32,1,160]{2,1,0:T(1,128)S(1)}, u32[]{:S(2)}, u32[]{:S(2)}) collective-permute-start(f32[32,1,160]{2,1,0:T(1,128)S(1)} %copy.60), channel_id=1, source_target_pairs={{4,0},{8,4},{12,8},{16,12},{20,16},{24,20},{28,24},{5,1},{9,5},{13... | collective-permute-start | bytes 61448 | tf_op jit(solution)/shard_map/ppermute | solution.py:20
  17.8 3.1 %collective-permute-start.1 = (f32[32,42,1]{1,0,2:T(8,128)S(1)}, f32[32,42,1]{1,0,2:T(8,128)S(1)}, u32[]{:S(2)}, u32[]{:S(2)}) collective-permute-start(f32[32,42,1]{1,0,2:T(8,128)S(1)} %pad_maximum_fusion.7), channel_id=1, source_target_pairs={{1,0},{2,1},{3,2},{5,4},{6,5},{7,6},{9,8},{10,9},{11,10},{13,12},{... | collective-permute-start | bytes 16136 | tf_op jit(solution)/shard_map/ppermute | solution.py:20
  23.8 3.1 %copy-start.11 = (f32[1,512,512]{2,1,0:T(8,128)S(1)}, f32[1,512,512]{2,1,0:T(8,128)}, u32[]{:S(2)}) copy-start(f32[1,512,512]{2,1,0:T(8,128)} %param.22) | copy-start | bytes 3145732
  26.9 4.4 %copy-start.8 = (f32[3,512]{1,0:T(4,128)S(1)}, f32[3,512]{1,0:T(4,128)}, u32[]{:S(2)}) copy-start(f32[3,512]{1,0:T(4,128)} %param.23) | copy-start | bytes 18436
  26.9 12.0 %copy-start.4 = (f32[3,3,32,128]{3,2,1,0:T(8,128)S(1)}, f32[3,3,32,128]{3,2,1,0:T(8,128)}, u32[]{:S(2)}) copy-start(f32[3,3,32,128]{3,2,1,0:T(8,128)} %param.18) | copy-start | bytes 442372
  31.4 22.5 %copy-start = (bf16[512,4096]{0,1:T(8,128)(2,1)}, bf16[512,4096]{0,1:T(8,128)(2,1)S(1)}, u32[]{:S(2)}) copy-start(bf16[512,4096]{0,1:T(8,128)(2,1)S(1)} %get-tuple-element.26) | copy-start | bytes 12582916
  32.6 6.4 %collective-permute-start.2 = (f32[3,1,128]{2,1,0:T(1,128)S(1)}, f32[3,1,128]{2,1,0:T(1,128)S(1)}, u32[]{:S(2)}, u32[]{:S(2)}) collective-permute-start(f32[3,1,128]{2,1,0:T(1,128)S(1)} %slice.162), channel_id=1, source_target_pairs={{4,0},{8,4},{12,8},{16,12},{20,16},{24,20},{28,24},{5,1},{9,5},{13... | collective-permute-start | bytes 4616 | tf_op jit(solution)/shard_map/ppermute | solution.py:20
  33.9 5.0 %collective-permute-start.4 = (f32[3,32,1]{2,1,0:T(8,128)S(1)}, f32[3,32,1]{2,1,0:T(8,128)S(1)}, u32[]{:S(2)}, u32[]{:S(2)}) collective-permute-start(f32[3,32,1]{2,1,0:T(8,128)S(1)} %bitcast.213), channel_id=1, source_target_pairs={{1,0},{2,1},{3,2},{5,4},{6,5},{7,6},{9,8},{10,9},{11,10},{13,12},{... | collective-permute-start | bytes 1160 | tf_op jit(solution)/shard_map/ppermute | solution.py:20
  39.1 9.8 %collective-permute-start.5 = (f32[3,32,1]{2,1,0:T(8,128)S(1)}, f32[3,32,1]{2,1,0:T(8,128)S(1)}, u32[]{:S(2)}, u32[]{:S(2)}) collective-permute-start(f32[3,32,1]{2,1,0:T(8,128)S(1)} %slice.167), channel_id=1, source_target_pairs={{0,1},{1,2},{2,3},{4,5},{5,6},{6,7},{8,9},{9,10},{10,11},{12,13},{... | collective-permute-start | bytes 1160 | tf_op jit(solution)/shard_map/ppermute | solution.py:20
  43.8 6.2 %collective-permute-start.3 = (f32[3,1,128]{2,1,0:T(1,128)S(1)}, f32[3,1,128]{2,1,0:T(1,128)S(1)}, u32[]{:S(2)}, u32[]{:S(2)}) collective-permute-start(f32[3,1,128]{2,1,0:T(1,128)S(1)} %slice.163), channel_id=1, source_target_pairs={{0,4},{4,8},{8,12},{12,16},{16,20},{20,24},{24,28},{1,5},{5,9},{9,... | collective-permute-start | bytes 4616 | tf_op jit(solution)/shard_map/ppermute | solution.py:20
  60.8 2.0 copy-start.1
  68.7 6.9 %collective-permute-start.6 = (f32[32,42,1]{1,0,2:T(8,128)S(1)}, f32[32,42,1]{1,0,2:T(8,128)S(1)}, u32[]{:S(2)}, u32[]{:S(2)}) collective-permute-start(f32[32,42,1]{1,0,2:T(8,128)S(1)} %pad_maximum_fusion.8), channel_id=1, source_target_pairs={{0,1},{1,2},{2,3},{4,5},{5,6},{6,7},{8,9},{9,10},{10,11},{12,13},{... | collective-permute-start | bytes 16136 | tf_op jit(solution)/shard_map/ppermute | solution.py:20
  73.6 57.0 %copy-start.5 = (f32[32,8,32]{2,1,0:T(8,128)S(1)}, f32[32,8,32]{2,1,0:T(8,128)}, u32[]{:S(2)}) copy-start(f32[32,8,32]{2,1,0:T(8,128)} %param.27) | copy-start | bytes 98308
  75.7 150.9 %copy-start.9 = (f32[3,512]{1,0:T(4,128)S(1)}, f32[3,512]{1,0:T(4,128)}, u32[]{:S(2)}) copy-start(f32[3,512]{1,0:T(4,128)} %param.33) | copy-start | bytes 18436
  75.7 150.9 %copy-start.10 = (f32[3,512]{1,0:T(4,128)S(1)}, f32[3,512]{1,0:T(4,128)}, u32[]{:S(2)}) copy-start(f32[3,512]{1,0:T(4,128)} %param.32) | copy-start | bytes 18436
  75.7 151.5 %copy-start.2 = (f32[1,512,512]{2,1,0:T(8,128)S(1)}, f32[1,512,512]{2,1,0:T(8,128)}, u32[]{:S(2)}) copy-start(f32[1,512,512]{2,1,0:T(8,128)} %param.31) | copy-start | bytes 3145732
  76.5 153.9 %copy-start.6 = (f32[512,64]{0,1:T(8,128)S(1)}, f32[512,64]{0,1:T(8,128)}, u32[]{:S(2)}) copy-start(f32[512,64]{0,1:T(8,128)} %param.29) | copy-start | bytes 393220
  76.5 153.8 %copy-start.7 = (f32[512,64]{0,1:T(8,128)S(1)}, f32[512,64]{0,1:T(8,128)}, u32[]{:S(2)}) copy-start(f32[512,64]{0,1:T(8,128)} %param.28) | copy-start | bytes 393220
  76.6 7.7 %collective-permute-start.7 = (f32[32,1,160]{2,1,0:T(1,128)S(1)}, f32[32,1,160]{2,1,0:T(1,128)S(1)}, u32[]{:S(2)}, u32[]{:S(2)}) collective-permute-start(f32[32,1,160]{2,1,0:T(1,128)S(1)} %fusion.80), channel_id=1, source_target_pairs={{0,4},{4,8},{8,12},{12,16},{16,20},{20,24},{24,28},{1,5},{5,9},{9,... | collective-permute-start | bytes 61448 | tf_op jit(solution)/shard_map/ppermute | solution.py:20
Sparse Core Ops, SparseCore 0:
  87.5 133.4 all-reduce.3
where the time goes:
time: 240 us; the launch traced here: 239 us
  waiting for transfers between devices  94.6 us (39%)
  blocking collectives  41.9 us (17%)
  matrix products  31.7 us (13%)
  starting transfers between devices  21.1 us (9%)
  between operations  19.8 us (8%)
  other arithmetic  17.7 us (7%)
  local copies, waits for them, and re-layouts  12.2 us (5%)
    psum x1, waiting for transfers between devices, shards(): lax.psum((grad_in, grad_mid, grad_out), ('row', 'col'))  86.2 us
    psum x1, blocking collectives, grid_total_sum(): return lax.psum(grid_local, ('row', 'col'))  41.9 us
    ppermute x8, starting transfers between devices, shifted(): return lax.ppermute(block, axis, route)  21.1 us
    dot_general x3, matrix products, contract_cols(): lax.dot_general(former, latter, (((1,), (1,)), ((), ())), preferred_eleme...  9.93 us
    div x5, other arithmetic, adam_step(): new_one / (1.0 - BETA_ONE ** ADAM_STEP)  9.62 us
    dot_general x3, matrix products, contract_rows(): lax.dot_general(former, latter, (((0,), (0,)), ((), ())), preferred_eleme...  8.45 us
    ppermute x8, waiting for transfers between devices, shifted(): return lax.ppermute(block, axis, route)  8.35 us
    dot_general x3, matrix products, matmul(): return jnp.dot(former, latter, preferred_element_type=jnp.float32)  6.85 us
  transfers between devices with their start and end apart: 9, of which 6 were waited for; matrix products, arithmetic and copies ran while one was open for 7% of the time, Pallas kernels for 0%

commit v1 on v0

--- a/solution.py
+++ b/solution.py
@@ -143,7 +143,11 @@
 
 
 def grid_total_sum(grid_local):
-    return lax.psum(grid_local, ("row", "col"))
+
+    def review_the_rows(z):
+        return jnp.sum(lax.all_gather(z, axis_name=("row", "col")), axis=0)
+
+    return review_the_rows(grid_local)
 
 
 def shards(

time: 240 us -> 248 us (1.033)
  matrix products: 31.7 us -> 36 us
    psum x1 -> x0, blocking collectives: 41.9 us -> none  [grid_total_sum(): return lax.psum(grid_local, ('row', 'col'))]
    unnamed x0 -> x1, blocking collectives: none -> 40.5 us
    unnamed x32 -> x36, local copies, waits for them, and re-layouts: 4.27 us -> 8.19 us
  transfers between devices with their start and end apart: 9 -> 9, of which waited for: 6 -> 6; matrix products, arithmetic and copies ran while one was open for 7% -> 6% of each run, Pallas kernels for 0% -> 0%
where the time goes in v1:
time: 248 us; the launch traced here: 247 us
  waiting for transfers between devices  95.6 us (39%)
  blocking collectives  40.5 us (16%)
  matrix products  36 us (15%)
  starting transfers between devices  21.5 us (9%)
  between operations  19.8 us (8%)
  other arithmetic  19 us (8%)
  local copies, waits for them, and re-layouts  14.6 us (6%)
    psum x1, waiting for transfers between devices, shards(): lax.psum((grad_in, grad_mid, grad_out), ('row', 'col'))  86 us
    unnamed x1, blocking collectives  40.5 us
    ppermute x8, starting transfers between devices, shifted(): return lax.ppermute(block, axis, route)  21.5 us
    dot_general x3, matrix products, contract_rows(): lax.dot_general(former, latter, (((0,), (0,)), ((), ())), preferred_eleme...  10.7 us
    dot_general x3, matrix products, contract_cols(): lax.dot_general(former, latter, (((1,), (1,)), ((), ())), preferred_eleme...  9.94 us
    div x5, other arithmetic, adam_step(): new_one / (1.0 - BETA_ONE ** ADAM_STEP)  9.71 us
    ppermute x8, waiting for transfers between devices, shifted(): return lax.ppermute(block, axis, route)  9.59 us
    dot_general x3, matrix products, matmul(): return jnp.dot(former, latter, preferred_element_type=jnp.float32)  8.91 us
  transfers between devices with their start and end apart: 9, of which 6 were waited for; matrix products, arithmetic and copies ran while one was open for 6% of the time, Pallas kernels for 0%

profile of v1, /device:TPU:0, one launch (start us, length us, event | category | flops | bytes accessed | tf_op | source)
XLA Modules:
  0.0 247.0 jit_solution(14858821211089982279)
XLA Ops:
  9.2 1.3 collective-permute-start
  10.5 1.3 fusion.148
  14.1 1.9 collective-permute-done
  17.8 1.3 collective-permute-start.1
  19.1 1.8 collective-permute-done.1
  21.6 2.2 fusion.14
  26.9 6.5 %fusion.5 = (bf16[512,4096]{0,1:T(8,128)(2,1)S(1)}, f32[4096,512]{1,0:T(8,128)}) fusion(f32[1,512,512]{2,1,0:T(8,128)S(1)} %copy-done.10, f32[4096,512]{1,0:T(8,128)S(1)} %fusion.82), kind=kOutput, calls=%fused_computation.10 | convolution fusion | flops 2168717312 | bytes 22020096 | tf_op jit(solution)/shard_map/dot_general | solution.py:80
  33.4 1.9 copy-done
  36.6 1.3 collective-permute-start.4
  37.9 1.3 collective-permute-start.2
  39.3 2.3 collective-permute-done.4
  41.6 2.6 %collective-permute-done.2 = f32[3,1,128]{2,1,0:T(1,128)S(1)} collective-permute-done((f32[3,1,128]{2,1,0:T(1,128)S(1)}, f32[3,1,128]{2,1,0:T(1,128)S(1)}, u32[]{:S(2)}, u32[]{:S(2)}) %collective-permute-start.2) | collective-permute-done | bytes 1568 | tf_op jit(solution)/shard_map/ppermute | solution.py:20
  44.4 3.5 %collective-permute-start.5 = (f32[3,32,1]{2,1,0:T(8,128)S(1)}, f32[3,32,1]{2,1,0:T(8,128)S(1)}, u32[]{:S(2)}, u32[]{:S(2)}) collective-permute-start(f32[3,32,1]{2,1,0:T(8,128)S(1)} %slice.167), channel_id=1, source_target_pairs={{0,1},{1,2},{2,3},{4,5},{5,6},{6,7},{8,9},{9,10},{10,11},{12,13},{... | collective-permute-start | bytes 1160 | tf_op jit(solution)/shard_map/ppermute | solution.py:20
  48.0 4.7 %collective-permute-start.3 = (f32[3,1,128]{2,1,0:T(1,128)S(1)}, f32[3,1,128]{2,1,0:T(1,128)S(1)}, u32[]{:S(2)}, u32[]{:S(2)}) collective-permute-start(f32[3,1,128]{2,1,0:T(1,128)S(1)} %slice.163), channel_id=1, source_target_pairs={{0,4},{4,8},{8,12},{12,16},{16,20},{20,24},{24,28},{1,5},{5,9},{9,... | collective-permute-start | bytes 4616 | tf_op jit(solution)/shard_map/ppermute | solution.py:20
  54.1 5.8 %fusion.1 = bf16[512,4096]{0,1:T(8,128)(2,1)S(1)} fusion(f32[4096,512]{1,0:T(8,128)} %get-tuple-element.27, bf16[3,4096]{1,0:T(4,128)(2,1)S(1)} %fusion.63, f32[3,512]{1,0:T(4,128)S(1)} %copy-done.7), kind=kOutput, calls=%fused_computation.3 | convolution fusion | flops 31458816 | bytes 12613632 | tf_op jit(solution)/shard_map/dot_general | solution.py:84
  59.9 3.4 %convolution_bitcast_fusion.1 = f32[1,512,512]{2,1,0:T(8,128)} fusion(bf16[512,4096]{0,1:T(8,128)(2,1)S(1)} %fusion.1, f32[4096,512]{1,0:T(8,128)S(1)} %bitcast.208), kind=kOutput, calls=%fused_computation.24 | convolution fusion | flops 2157969408 | bytes 13631488 | tf_op jit(solution)/shard_map/dot_general | solution.py:90
  63.3 3.6 %fusion = bf16[512,4096]{0,1:T(8,128)(2,1)S(1)} fusion(f32[4096,512]{1,0:T(8,128)S(1)} %bitcast.208, bf16[512,4096]{0,1:T(8,128)(2,1)S(1)} %fusion.1, f32[1,512,512]{2,1,0:T(8,128)S(1)} %copy-done.10), kind=kOutput, calls=%fused_computation.1 | convolution fusion | flops 2166620160 | bytes 17825792 | tf_op jit(solution)/shard_map/dot_general | solution.py:84
  66.9 1.9 copy-done.1
  68.9 1.4 convolution_bitcast_fusion
  76.0 3.9 %collective-permute-start.6 = (f32[32,42,1]{1,0,2:T(8,128)S(1)}, f32[32,42,1]{1,0,2:T(8,128)S(1)}, u32[]{:S(2)}, u32[]{:S(2)}) collective-permute-start(f32[32,42,1]{1,0,2:T(8,128)S(1)} %pad_maximum_fusion.8), channel_id=1, source_target_pairs={{0,1},{1,2},{2,3},{4,5},{5,6},{6,7},{8,9},{9,10},{10,11},{12,13},{... | collective-permute-start | bytes 16136 | tf_op jit(solution)/shard_map/ppermute | solution.py:20
  79.9 3.7 %fusion.150 = f32[512,64]{0,1:T(8,128)} fusion(bf16[64,4096]{1,0:T(8,128)(2,1)S(1)} %bitcast_dynamic-update-slice_fusion, bf16[512,4096]{0,1:T(8,128)(2,1)} %copy-done.1), kind=kOutput, calls=%fused_computation.235 | convolution fusion | flops 268435456 | bytes 4849664 | tf_op jit(solution)/shard_map/dot_general | solution.py:90
  85.6 4.1 %collective-permute-start.7 = (f32[32,1,160]{2,1,0:T(1,128)S(1)}, f32[32,1,160]{2,1,0:T(1,128)S(1)}, u32[]{:S(2)}, u32[]{:S(2)}) collective-permute-start(f32[32,1,160]{2,1,0:T(1,128)S(1)} %fusion.80), channel_id=1, source_target_pairs={{0,4},{4,8},{8,12},{12,16},{16,20},{20,24},{24,28},{1,5},{5,9},{9,... | collective-permute-start | bytes 61448 | tf_op jit(solution)/shard_map/ppermute | solution.py:20
  89.7 2.8 %fusion.149 = f32[3,512]{1,0:T(4,128)S(1)} fusion(bf16[3,4096]{1,0:T(4,128)(2,1)S(1)} %fusion.63, bf16[512,4096]{0,1:T(8,128)(2,1)} %copy-done), kind=kOutput, calls=%fused_computation.234 | convolution fusion | flops 12582912 | bytes 4225024 | tf_op jit(solution)/shard_map/dot_general | solution.py:90
  92.6 1.4 multiply_reduce_fusion.3
  96.4 40.5 %all-reduce.1 = (f32[32]{0:T(128)S(1)}, f32[3,512]{1,0:T(4,128)S(1)}) all-reduce(f32[32]{0:T(128)S(1)} %dynamic-update-slice, f32[3,512]{1,0:T(4,128)S(1)} %fusion.149), channel_id=1, replica_groups=mesh['row'=8,'col'=4] {'row','col'}, use_global_device_ids=true, to_apply=%add | all-reduce | flops 1568 | bytes 12544
  138.9 1.8 fusion.49
  140.7 2.3 fusion.29
  143.0 86.0 %all-reduce.5.cloned.1.call-done = (f32[512,64]{0,1:T(8,128)}, f32[1,512,512]{2,1,0:T(8,128)}) async-done(((f32[512,64]{0,1:T(8,128)}, f32[1,512,512]{2,1,0:T(8,128)}), (f32[512,64]{0,1:T(8,128)}, f32[1,512,512]{2,1,0:T(8,128)})) %all-reduce.5.cloned.1.call-update) | async-done | bytes 1179664 | tf_op jit(solution)/shard_map/psum | solution.py:254
  229.0 2.1 multiply_reduce_fusion
  231.1 1.5 multiply_reduce_fusion.2
  235.2 3.2 %fusion.24 = f32[1,512,512]{2,1,0:T(8,128)} fusion(f32[1,512,512]{2,1,0:T(8,128)S(1)} %copy-done.3, f32[1,512,512]{2,1,0:T(8,128)} %get-tuple-element.8, f32[1,512,512]{2,1,0:T(8,128)} %param.30, f32[]{:T(128)S(6)} %min.7), kind=kLoop, calls=%fused_computation.39 | loop fusion | flops 3145728 | bytes 4194308 | tf_op jit(solution)/shard_map/div | solution.py:139
  238.4 1.8 fusion.54
  (103 shorter events, 22.0 us)
Async XLA Ops:
  7.2 18.4 %copy-start.4 = (f32[512,64]{0,1:T(8,128)S(1)}, f32[512,64]{0,1:T(8,128)}, u32[]{:S(2)}) copy-start(f32[512,64]{0,1:T(8,128)} %param.21) | copy-start | bytes 393220
  7.2 221.8 %all-reduce.5.cloned.1.call-start = ((), (), s32[]{:S(2)}) async-start(), calls=%async_computation | async-start | bytes 2359296 | tf_op jit(solution)/shard_map/psum | solution.py:254
  9.2 6.8 %collective-permute-start = (f32[32,1,160]{2,1,0:T(1,128)S(1)}, f32[32,1,160]{2,1,0:T(1,128)S(1)}, u32[]{:S(2)}, u32[]{:S(2)}) collective-permute-start(f32[32,1,160]{2,1,0:T(1,128)S(1)} %copy.60), channel_id=1, source_target_pairs={{4,0},{8,4},{12,8},{16,12},{20,16},{24,20},{28,24},{5,1},{9,5},{13... | collective-permute-start | bytes 61448 | tf_op jit(solution)/shard_map/ppermute | solution.py:20
  17.8 3.1 %collective-permute-start.1 = (f32[32,42,1]{1,0,2:T(8,128)S(1)}, f32[32,42,1]{1,0,2:T(8,128)S(1)}, u32[]{:S(2)}, u32[]{:S(2)}) collective-permute-start(f32[32,42,1]{1,0,2:T(8,128)S(1)} %pad_maximum_fusion.7), channel_id=1, source_target_pairs={{1,0},{2,1},{3,2},{5,4},{6,5},{7,6},{9,8},{10,9},{11,10},{13,12},{... | collective-permute-start | bytes 16136 | tf_op jit(solution)/shard_map/ppermute | solution.py:20
  23.8 3.1 %copy-start.10 = (f32[1,512,512]{2,1,0:T(8,128)S(1)}, f32[1,512,512]{2,1,0:T(8,128)}, u32[]{:S(2)}) copy-start(f32[1,512,512]{2,1,0:T(8,128)} %param.22) | copy-start | bytes 3145732
  26.9 6.5 %copy-start.2 = (f32[4096,512]{1,0:T(8,128)}, f32[4096,512]{1,0:T(8,128)S(1)}, u32[]{:S(2)}) copy-start(f32[4096,512]{1,0:T(8,128)S(1)} %fusion.82) | copy-start | bytes 25165828
  26.9 8.4 %copy-start.7 = (f32[3,512]{1,0:T(4,128)S(1)}, f32[3,512]{1,0:T(4,128)}, u32[]{:S(2)}) copy-start(f32[3,512]{1,0:T(4,128)} %param.23) | copy-start | bytes 18436
  26.9 17.3 %copy-start.6 = (f32[3,3,32,128]{3,2,1,0:T(8,128)S(1)}, f32[3,3,32,128]{3,2,1,0:T(8,128)}, u32[]{:S(2)}) copy-start(f32[3,3,32,128]{3,2,1,0:T(8,128)} %param.18) | copy-start | bytes 442372
  33.4 2.0 copy-start
  36.6 5.0 %collective-permute-start.4 = (f32[3,32,1]{2,1,0:T(8,128)S(1)}, f32[3,32,1]{2,1,0:T(8,128)S(1)}, u32[]{:S(2)}, u32[]{:S(2)}) collective-permute-start(f32[3,32,1]{2,1,0:T(8,128)S(1)} %bitcast.216), channel_id=1, source_target_pairs={{1,0},{2,1},{3,2},{5,4},{6,5},{7,6},{9,8},{10,9},{11,10},{13,12},{... | collective-permute-start | bytes 1160 | tf_op jit(solution)/shard_map/ppermute | solution.py:20
  37.9 6.4 %collective-permute-start.2 = (f32[3,1,128]{2,1,0:T(1,128)S(1)}, f32[3,1,128]{2,1,0:T(1,128)S(1)}, u32[]{:S(2)}, u32[]{:S(2)}) collective-permute-start(f32[3,1,128]{2,1,0:T(1,128)S(1)} %slice.162), channel_id=1, source_target_pairs={{4,0},{8,4},{12,8},{16,12},{20,16},{24,20},{28,24},{5,1},{9,5},{13... | collective-permute-start | bytes 4616 | tf_op jit(solution)/shard_map/ppermute | solution.py:20
  44.4 8.3 %collective-permute-start.5 = (f32[3,32,1]{2,1,0:T(8,128)S(1)}, f32[3,32,1]{2,1,0:T(8,128)S(1)}, u32[]{:S(2)}, u32[]{:S(2)}) collective-permute-start(f32[3,32,1]{2,1,0:T(8,128)S(1)} %slice.167), channel_id=1, source_target_pairs={{0,1},{1,2},{2,3},{4,5},{5,6},{6,7},{8,9},{9,10},{10,11},{12,13},{... | collective-permute-start | bytes 1160 | tf_op jit(solution)/shard_map/ppermute | solution.py:20
  48.0 5.8 %collective-permute-start.3 = (f32[3,1,128]{2,1,0:T(1,128)S(1)}, f32[3,1,128]{2,1,0:T(1,128)S(1)}, u32[]{:S(2)}, u32[]{:S(2)}) collective-permute-start(f32[3,1,128]{2,1,0:T(1,128)S(1)} %slice.163), channel_id=1, source_target_pairs={{0,4},{4,8},{8,12},{12,16},{16,20},{20,24},{24,28},{1,5},{5,9},{9,... | collective-permute-start | bytes 4616 | tf_op jit(solution)/shard_map/ppermute | solution.py:20
  53.8 6.1 %slice-start = ((s8[8388608]{0:T(1024)(128)(4,1)}), s8[4194304]{0:T(1024)(128)(4,1)S(1)}, s32[]{:S(2)}) async-start(s8[8388608]{0:T(1024)(128)(4,1)} %bitcast.207), calls=%async_computation.1 | async-start | bytes 8388608
  54.1 5.8 %slice-start.1 = ((s8[8388608]{0:T(1024)(128)(4,1)}), s8[4194304]{0:T(1024)(128)(4,1)S(1)}, s32[]{:S(2)}) async-start(s8[8388608]{0:T(1024)(128)(4,1)} %bitcast.207), calls=%async_computation.2 | async-start | bytes 8388608
  66.9 2.0 copy-start.1
  76.0 8.7 %collective-permute-start.6 = (f32[32,42,1]{1,0,2:T(8,128)S(1)}, f32[32,42,1]{1,0,2:T(8,128)S(1)}, u32[]{:S(2)}, u32[]{:S(2)}) collective-permute-start(f32[32,42,1]{1,0,2:T(8,128)S(1)} %pad_maximum_fusion.8), channel_id=1, source_target_pairs={{0,1},{1,2},{2,3},{4,5},{5,6},{6,7},{8,9},{9,10},{10,11},{12,13},{... | collective-permute-start | bytes 16136 | tf_op jit(solution)/shard_map/ppermute | solution.py:20
  83.6 57.1 %copy-start.5 = (f32[32,32,128]{2,1,0:T(8,128)S(1)}, f32[32,32,128]{2,1,0:T(8,128)}, u32[]{:S(2)}) copy-start(f32[32,32,128]{2,1,0:T(8,128)} %param.25) | copy-start | bytes 1572868
  84.7 149.8 %copy-start.8 = (f32[3,512]{1,0:T(4,128)S(1)}, f32[3,512]{1,0:T(4,128)}, u32[]{:S(2)}) copy-start(f32[3,512]{1,0:T(4,128)} %param.33) | copy-start | bytes 18436
  84.7 149.9 %copy-start.9 = (f32[3,512]{1,0:T(4,128)S(1)}, f32[3,512]{1,0:T(4,128)}, u32[]{:S(2)}) copy-start(f32[3,512]{1,0:T(4,128)} %param.32) | copy-start | bytes 18436
  84.7 150.5 %copy-start.3 = (f32[1,512,512]{2,1,0:T(8,128)S(1)}, f32[1,512,512]{2,1,0:T(8,128)}, u32[]{:S(2)}) copy-start(f32[1,512,512]{2,1,0:T(8,128)} %param.31) | copy-start | bytes 3145732
  85.6 6.9 %collective-permute-start.7 = (f32[32,1,160]{2,1,0:T(1,128)S(1)}, f32[32,1,160]{2,1,0:T(1,128)S(1)}, u32[]{:S(2)}, u32[]{:S(2)}) collective-permute-start(f32[32,1,160]{2,1,0:T(1,128)S(1)} %fusion.80), channel_id=1, source_target_pairs={{0,4},{4,8},{8,12},{12,16},{16,20},{20,24},{24,28},{1,5},{5,9},{9,... | collective-permute-start | bytes 61448 | tf_op jit(solution)/shard_map/ppermute | solution.py:20
Sparse Core Ops, SparseCore 0:
  96.5 132.4 all-reduce.4
